TPU v7x, 512 devices: a whole 4x8x8 slice. The times are simulated.
512 devices in a mesh: probe: 4 (over x), seq: 128 (over y, z, core).
Axes of the slice: x: 4, y: 8, z: 8, core: 2. Of those that a mesh axis runs over, the one named last changes fastest.
Arguments:
- probe_bits: int32 [4, 128, 16384], P('probe', 'seq'), may hold values from 0 to 1
- noise_var: float32 [128, 16384], P('seq'), may hold values from 0.2 to 12
- kernel_spectrum: float32 [16384, 128], P('seq'), may hold values from 0.05 to 4, as said below
- symbol: float32 [16384, 128], P('seq'), may hold values from 0.3 to 3, as said below
- grad_prev: float32 [16384, 128], P('seq', 'probe'), may hold values from -6 to 6
Outputs:
- residual: float32 [4, 128, 16384], P('probe', 'seq')
- grad_total: float32 [16384, 128], P('seq', 'probe')
Inputs may be any that keep to these rules, and one draw needn't show every extreme that they name: kernel_spectrum at frequency k equals kernel_spectrum at frequency (2097152 - k) mod 2097152. symbol at frequency k equals symbol at frequency (2097152 - k) mod 2097152.
All inputs are finite; a program needn't handle non-finite values.
Results may differ from a plain program's by a relative error of at most 0.00017.
Values sent between devices are 32-bit elements; how exact they have to be, the bound alone decides.
A program may use at most 64 MiB of HBM per device.

v0:
```python
import math
import jax
import jax.numpy as jnp
from jax import lax
from jax.sharding import PartitionSpec as P

highest = lax.Precision.HIGHEST
minor_width = 128


def dft_table(height, breadth, modulus, orient):
    left_index = jnp.arange(height, dtype=jnp.int32)[:, None]
    right_index = jnp.arange(breadth, dtype=jnp.int32)[None, :]
    phases = (
        orient * 2.0 * math.pi / modulus * (left_index * right_index % modulus).astype(jnp.float32)
    )
    return (jnp.cos(phases), jnp.sin(phases))


def complex_product(pattern, real_part, imaginary, cosine_table, sine_table):
    real_cos = jnp.einsum(pattern, real_part, cosine_table, precision=highest)
    real_sin = jnp.einsum(pattern, real_part, sine_table, precision=highest)
    if imaginary is None:
        return (real_cos, real_sin)
    imag_cos = jnp.einsum(pattern, imaginary, cosine_table, precision=highest)
    imag_sin = jnp.einsum(pattern, imaginary, sine_table, precision=highest)
    return (real_cos - imag_sin, real_sin + imag_cos)


def rotate(real_part, imaginary, cosine_table, sine_table):
    return (
        real_part * cosine_table - imaginary * sine_table,
        real_part * sine_table + imaginary * cosine_table,
    )


def forward_rows(series):
    major_len = series.shape[-2]
    length = major_len * minor_width
    cosine_table, sine_table = dft_table(major_len, major_len, major_len, -1.0)
    section_real, section_imag = complex_product(
        "...mi,mk->...ik", series, None, cosine_table, sine_table
    )
    turn_cos, turn_sin = dft_table(minor_width, major_len, length, -1.0)
    twisted_real, twisted_imag = rotate(section_real, section_imag, turn_cos, turn_sin)
    cosine_table, sine_table = dft_table(minor_width, minor_width, minor_width, -1.0)
    return complex_product("...ik,ij->...jk", twisted_real, twisted_imag, cosine_table, sine_table)


def inverse_rows(real_part, imaginary):
    major_len = real_part.shape[-1]
    length = major_len * minor_width
    cosine_table, sine_table = dft_table(minor_width, minor_width, minor_width, 1.0)
    section_real, section_imag = complex_product(
        "...jk,ji->...ik", real_part, imaginary, cosine_table, sine_table
    )
    turn_cos, turn_sin = dft_table(minor_width, major_len, length, 1.0)
    twisted_real, twisted_imag = rotate(section_real, section_imag, turn_cos, turn_sin)
    cosine_table, sine_table = dft_table(major_len, major_len, major_len, 1.0)
    final_real, unused = complex_product(
        "...ik,km->...mi", twisted_real, twisted_imag, cosine_table, sine_table
    )
    return final_real


def global_twiddle(local_rows, major_len, samples, orient):
    row_index = lax.axis_index("seq") * local_rows + jnp.arange(local_rows, dtype=jnp.int32)
    column_index = (
        jnp.arange(minor_width, dtype=jnp.int32)[:, None] * major_len
        + jnp.arange(major_len, dtype=jnp.int32)[None, :]
    )
    phases = (
        orient
        * 2.0
        * math.pi
        / samples
        * (row_index[:, None, None] * column_index[None, :, :] % samples).astype(jnp.float32)
    )
    return (jnp.cos(phases), jnp.sin(phases))


def forward_spectrum(series):
    local_rows = series.shape[1]
    major_len = series.shape[2]
    devices = lax.axis_size("seq")
    all_rows = local_rows * devices
    samples = all_rows * major_len * minor_width
    real_part, imaginary = forward_rows(series)
    turn_cos, turn_sin = global_twiddle(local_rows, major_len, samples, -1.0)
    turned_real, turned_imag = rotate(real_part, imaginary, turn_cos, turn_sin)
    arrived = lax.all_to_all(
        jnp.stack([turned_real, turned_imag]), "seq", split_axis=3, concat_axis=2, tiled=True
    )
    block = minor_width // devices * major_len
    arrived = arrived.reshape(arrived.shape[0], arrived.shape[1], all_rows, block)
    cosine_table, sine_table = dft_table(all_rows, all_rows, all_rows, -1.0)
    return complex_product("zrb,ra->zba", arrived[0], arrived[1], cosine_table, sine_table)


def inverse_field(spectrum_real, spectrum_imag):
    all_rows = spectrum_real.shape[2]
    block = spectrum_real.shape[1]
    devices = lax.axis_size("seq")
    major_len = block * devices // minor_width
    cosine_table, sine_table = dft_table(all_rows, all_rows, all_rows, 1.0)
    back_real, back_imag = complex_product(
        "zba,ar->zrb", spectrum_real, spectrum_imag, cosine_table, sine_table
    )
    stacked = jnp.stack([back_real, back_imag])
    stacked = stacked.reshape(
        stacked.shape[0], stacked.shape[1], all_rows, minor_width // devices, major_len
    )
    arrived = lax.all_to_all(stacked, "seq", split_axis=2, concat_axis=3, tiled=True)
    local_rows = arrived.shape[2]
    samples = all_rows * major_len * minor_width
    turn_cos, turn_sin = global_twiddle(local_rows, major_len, samples, 1.0)
    turned_real, turned_imag = rotate(arrived[0], arrived[1], turn_cos, turn_sin)
    return inverse_rows(turned_real, turned_imag) / samples


def shards(probe_bits, noise_var, kernel_spectrum, symbol, grad_prev):
    field_shape = (
        probe_bits.shape[0],
        probe_bits.shape[1],
        probe_bits.shape[2] // minor_width,
        minor_width,
    )
    sign_field = (2 * probe_bits - 1).astype(jnp.float32).reshape(field_shape)
    noise_field = noise_var.reshape(field_shape[1:])
    samples = kernel_spectrum.shape[1] * noise_var.shape[1]
    base_real, base_imag = forward_spectrum(sign_field)
    scaled_real = base_real / symbol
    scaled_imag = base_imag / symbol
    precond = inverse_field(scaled_real, scaled_imag)
    again_real, again_imag = forward_spectrum(precond)
    circulant = inverse_field(kernel_spectrum * again_real, kernel_spectrum * again_imag)
    kernel_image = circulant + noise_field * precond
    numerator, curvature = lax.psum(
        (jnp.sum(sign_field * precond), jnp.sum(precond * kernel_image)), "seq"
    )
    step_size = numerator / curvature
    residual = sign_field - step_size * kernel_image
    cross_term = lax.psum(jnp.sum(residual * kernel_image), "seq")
    weight = -2.0 * cross_term
    resid_real, resid_imag = forward_spectrum(residual)
    applied = (
        inverse_field(kernel_spectrum * resid_real, kernel_spectrum * resid_imag)
        + noise_field * residual
    )
    adjoint = (
        weight / curvature * sign_field
        - 2.0 * weight * step_size / curvature * kernel_image
        - 2.0 * step_size * applied
    )
    adjoint_real, adjoint_imag = forward_spectrum(adjoint)
    local_grad = -(adjoint_real[0] * base_real[0] + adjoint_imag[0] * base_imag[0]) / (
        samples * symbol * symbol
    )
    probes = lax.axis_size("probe")
    summed = lax.psum(local_grad, "probe")
    share_width = summed.shape[1] // probes
    own_share = lax.dynamic_slice_in_dim(
        summed, lax.axis_index("probe") * share_width, share_width, 1
    )
    grad_total = grad_prev + own_share / probes
    return (residual.reshape(probe_bits.shape), grad_total)


def solution(mesh):
    placed = (
        P("probe", "seq", None),
        P("seq", None),
        P("seq", None),
        P("seq", None),
        P("seq", "probe"),
    )
    return jax.shard_map(
        shards,
        mesh=mesh,
        in_specs=placed,
        out_specs=(P("probe", "seq", None), P("seq", "probe")),
        check_vma=False,
    )
```

profile of v0, /device:TPU:8, one launch (start us, length us, event | category | flops | bytes accessed | tf_op | source)
XLA Modules:
  0.0 741.7 jit_solution(7742233880407343323)
XLA Ops:
  7.2 0.9 add_convert_fusion
  11.2 0.9 subtract_bitcast_fusion.3
  12.2 29.0 %all_to_all.28 = f32[2,1,1,128,128]{4,2,1,0,3:T(1,128)S(1)} all-to-all(f32[2,1,1,128,128]{4,2,1,0,3:T(1,128)S(1)} %copy.13), channel_id=1, replica_groups=mesh['probe'=4,'seq'=128] {'seq'}, dimensions={3} | all-to-all | bytes 262144 | tf_op jit(solution)/shard_map/all_to_all | solution.py:91
  45.9 18.2 %all_to_all.29 = f32[2,1,128,1,128]{4,3,1,0,2:T(1,128)S(1)} all-to-all(f32[2,1,128,1,128]{4,3,1,0,2:T(1,128)S(1)} %copy.14), channel_id=1, replica_groups=mesh['probe'=4,'seq'=128] {'seq'}, dimensions={2} | all-to-all | bytes 262144 | tf_op jit(solution)/shard_map/all_to_all | solution.py:113
  67.1 0.8 fusion.43
  67.9 0.8 fusion.16
  71.7 0.9 subtract_bitcast_fusion.2
  72.8 18.1 %all_to_all.30 = f32[2,1,1,128,128]{4,2,1,0,3:T(1,128)S(1)} all-to-all(f32[2,1,1,128,128]{4,2,1,0,3:T(1,128)S(1)} %copy.17), channel_id=1, replica_groups=mesh['probe'=4,'seq'=128] {'seq'}, dimensions={3} | all-to-all | bytes 262144 | tf_op jit(solution)/shard_map/all_to_all | solution.py:91
  95.5 17.8 %all_to_all.31 = f32[2,1,128,1,128]{4,3,1,0,2:T(1,128)S(1)} all-to-all(f32[2,1,128,1,128]{4,3,1,0,2:T(1,128)S(1)} %copy.18), channel_id=1, replica_groups=mesh['probe'=4,'seq'=128] {'seq'}, dimensions={2} | all-to-all | bytes 262144 | tf_op jit(solution)/shard_map/all_to_all | solution.py:113
  116.4 0.8 fusion.36
  117.2 1.4 multiply_reduce_fusion.1
  118.6 213.3 %all-reduce = (f32[]{:T(128)}, f32[]{:T(128)}) all-reduce(f32[]{:T(128)} %get-tuple-element.7, f32[]{:T(128)} %get-tuple-element.6), channel_id=1, replica_groups=mesh['probe'=4,'seq'=128] {'seq'}, use_global_device_ids=true, to_apply=%region_1.2 | all-reduce | flops 2 | bytes 16 | tf_op jit(solution)/shard_map/psum | solution.py:138
  337.0 0.9 subtract_bitcast_fusion.1
  338.0 53.9 %all_to_all.32 = f32[2,1,1,128,128]{4,2,1,0,3:T(1,128)S(1)} all-to-all(f32[2,1,1,128,128]{4,2,1,0,3:T(1,128)S(1)} %copy.21), channel_id=1, replica_groups=mesh['probe'=4,'seq'=128] {'seq'}, dimensions={3} | all-to-all | bytes 262144 | tf_op jit(solution)/shard_map/all_to_all | solution.py:91
  396.0 0.8 copy.22
  396.8 6.6 all-to-all-start.5
  403.4 217.7 %psum.30 = f32[]{:T(128)} all-reduce(f32[]{:T(128)} %get-tuple-element.10), channel_id=1, replica_groups=mesh['probe'=4,'seq'=128] {'seq'}, use_global_device_ids=true, to_apply=%region_5.6 | all-reduce | flops 1 | bytes 8 | tf_op jit(solution)/shard_map/psum | solution.py:143
  626.9 0.8 fusion.29
  627.7 0.8 fusion.20
  631.5 0.9 subtract_bitcast_fusion
  632.6 53.0 %all_to_all.33 = f32[2,1,1,128,128]{4,2,1,0,3:T(1,128)S(1)} all-to-all(f32[2,1,1,128,128]{4,2,1,0,3:T(1,128)S(1)} %copy.25), channel_id=1, replica_groups=mesh['probe'=4,'seq'=128] {'seq'}, dimensions={3} | all-to-all | bytes 262144 | tf_op jit(solution)/shard_map/all_to_all | solution.py:91
  687.1 1.1 fusion.21
  689.0 44.0 %all-reduce.3.cloned.1.call-done = f32[128,128]{1,0:T(8,128)} async-done(((f32[128,128]{1,0:T(8,128)}), f32[128,128]{1,0:T(8,128)}) %all-reduce.3.cloned.1.call-update) | async-done | bytes 65552 | tf_op jit(solution)/shard_map/psum | solution.py:160
  733.0 0.9 multiply_add_fusion
  (96 shorter events, 38.6 us)
Async XLA Ops:
  42.3 0.8 copy-start.4
  91.4 0.8 copy-start.2
  116.4 0.8 copy-start.3
  333.9 293.8 %copy-start = (f32[128,128]{1,0:T(8,128)}, f32[128,128]{1,0:T(8,128)S(1)}, u32[]{:S(2)}) copy-start(f32[128,128]{1,0:T(8,128)S(1)} %get-tuple-element.11) | copy-start | bytes 196612
  396.8 227.0 %all-to-all-start.5 = ((f32[2,1,128,1,128]{4,3,1,0,2:T(1,128)}), f32[2,1,128,1,128]{4,3,1,0,2:T(1,128)S(1)}, u32[]{:S(2)}, u32[]{:S(2)}) async-start(f32[2,1,128,1,128]{4,3,1,0,2:T(1,128)} %copy.22), calls=%async_computation.5 | async-start | bytes 262144 | tf_op jit(solution)/shard_map/all_to_all | solution.py:113
  403.4 329.7 %all-reduce.3.cloned.1.call-start = ((), (), s32[]{:S(2)}) async-start(), calls=%async_computation.7 | async-start | bytes 131072 | tf_op jit(solution)/shard_map/psum | solution.py:160
  688.2 0.7 copy-start.1
Sparse Core Ops, SparseCore 0:
  688.3 44.6 all-reduce.2
where the time goes:
time: 750 us; the launch traced here: 742 us
  blocking collectives  621 us (83%)
  waiting for transfers between devices  44.1 us (6%)
  matrix products  43.9 us (6%)
  between operations  18.9 us (3%)
    psum x1, blocking collectives, shards(): cross_term = lax.psum(jnp.sum(residual * kernel_image), 'seq')  218 us
    psum x1, blocking collectives, shards(): lax.psum((jnp.sum(sign_field * precond), jnp.sum(precond * kernel_image))...  213 us
    all_to_all x4, blocking collectives, forward_spectrum(): lax.all_to_all(jnp.stack([turned_real, turned_imag]), 'seq', split_axis=3...  154 us
    psum x1, waiting for transfers between devices, shards(): summed = lax.psum(local_grad, 'probe')  44 us
    all_to_all x2, blocking collectives, inverse_field(): lax.all_to_all(stacked, 'seq', split_axis=2, concat_axis=3, tiled=True)  36 us
  transfers between devices with their start and end apart: 2, of which 1 were waited for; matrix products, arithmetic and copies ran while one was open for 0% of the time, Pallas kernels for 0%

commit v1 on v0

--- a/solution.py
+++ b/solution.py
@@ -6,6 +6,10 @@
 
 highest = lax.Precision.HIGHEST
 minor_width = 128
+
+
+def divide_weights(frame_in):
+    return lax.all_gather(frame_in, "probe").sum(axis=0)
 
 
 def dft_table(height, breadth, modulus, orient):
@@ -157,7 +161,7 @@
         samples * symbol * symbol
     )
     probes = lax.axis_size("probe")
-    summed = lax.psum(local_grad, "probe")
+    summed = divide_weights(local_grad)
     share_width = summed.shape[1] // probes
     own_share = lax.dynamic_slice_in_dim(
         summed, lax.axis_index("probe") * share_width, share_width, 1

time: 750 us -> 705 us (0.940)
  the two profiles are of different devices: /device:TPU:8 before, /device:TPU:2 now
where the time goes in v1:
time: 705 us; the launch traced here: 696 us
  blocking collectives  616 us (87%)
  matrix products  43.2 us (6%)
  starting transfers between devices  12.6 us (2%)
  waiting for transfers between devices  12.2 us (2%)
    psum x1, blocking collectives, shards(): cross_term = lax.psum(jnp.sum(residual * kernel_image), 'seq')  253 us
    psum x1, blocking collectives, shards(): lax.psum((jnp.sum(sign_field * precond), jnp.sum(precond * kernel_image))...  248 us
    all_to_all x3, blocking collectives, forward_spectrum(): lax.all_to_all(jnp.stack([turned_real, turned_imag]), 'seq', split_axis=3...  67.4 us
    all_to_all x2, blocking collectives, inverse_field(): lax.all_to_all(stacked, 'seq', split_axis=2, concat_axis=3, tiled=True)  35.9 us
  transfers between devices with their start and end apart: 2, of which 1 were waited for; matrix products, arithmetic and copies ran while one was open for 0% of the time, Pallas kernels for 0%

profile of v1, /device:TPU:2, one launch (start us, length us, event | category | flops | bytes accessed | tf_op | source)
XLA Modules:
  0.0 696.3 jit_solution(2999850474396409225)
XLA Ops:
  0.6 0.9 add_convert_fusion
  4.6 0.9 subtract_bitcast_fusion.3
  5.7 29.9 %all_to_all.28 = f32[2,1,1,128,128]{4,2,1,0,3:T(1,128)S(1)} all-to-all(f32[2,1,1,128,128]{4,2,1,0,3:T(1,128)S(1)} %copy.7), channel_id=1, replica_groups=mesh['probe'=4,'seq'=128] {'seq'}, dimensions={3} | all-to-all | bytes 262144 | tf_op jit(solution)/shard_map/all_to_all | solution.py:95
  40.2 18.1 %all_to_all.29 = f32[2,1,128,1,128]{4,3,1,0,2:T(1,128)S(1)} all-to-all(f32[2,1,128,1,128]{4,3,1,0,2:T(1,128)S(1)} %copy.8), channel_id=1, replica_groups=mesh['probe'=4,'seq'=128] {'seq'}, dimensions={2} | all-to-all | bytes 262144 | tf_op jit(solution)/shard_map/all_to_all | solution.py:117
  61.4 0.8 fusion.43
  62.1 0.8 fusion.16
  66.0 0.9 subtract_bitcast_fusion.2
  67.0 18.1 %all_to_all.30 = f32[2,1,1,128,128]{4,2,1,0,3:T(1,128)S(1)} all-to-all(f32[2,1,1,128,128]{4,2,1,0,3:T(1,128)S(1)} %copy.11), channel_id=1, replica_groups=mesh['probe'=4,'seq'=128] {'seq'}, dimensions={3} | all-to-all | bytes 262144 | tf_op jit(solution)/shard_map/all_to_all | solution.py:95
  89.7 17.8 %all_to_all.31 = f32[2,1,128,1,128]{4,3,1,0,2:T(1,128)S(1)} all-to-all(f32[2,1,128,1,128]{4,3,1,0,2:T(1,128)S(1)} %copy.12), channel_id=1, replica_groups=mesh['probe'=4,'seq'=128] {'seq'}, dimensions={2} | all-to-all | bytes 262144 | tf_op jit(solution)/shard_map/all_to_all | solution.py:117
  110.7 0.8 fusion.36
  111.5 1.4 multiply_reduce_fusion.1
  112.9 248.0 %all-reduce = (f32[]{:T(128)}, f32[]{:T(128)}) all-reduce(f32[]{:T(128)} %get-tuple-element.5, f32[]{:T(128)} %get-tuple-element.4), channel_id=1, replica_groups=mesh['probe'=4,'seq'=128] {'seq'}, use_global_device_ids=true, to_apply=%region_1.2 | all-reduce | flops 2 | bytes 16 | tf_op jit(solution)/shard_map/psum | solution.py:142
  365.9 0.9 subtract_bitcast_fusion.1
  366.9 19.3 %all_to_all.32 = f32[2,1,1,128,128]{4,2,1,0,3:T(1,128)S(1)} all-to-all(f32[2,1,1,128,128]{4,2,1,0,3:T(1,128)S(1)} %copy.15), channel_id=1, replica_groups=mesh['probe'=4,'seq'=128] {'seq'}, dimensions={3} | all-to-all | bytes 262144 | tf_op jit(solution)/shard_map/all_to_all | solution.py:95
  390.3 0.8 copy.16
  391.1 6.2 all-to-all-start.5
  397.2 252.7 %psum.23 = f32[]{:T(128)} all-reduce(f32[]{:T(128)} %get-tuple-element.8), channel_id=1, replica_groups=mesh['probe'=4,'seq'=128] {'seq'}, use_global_device_ids=true, to_apply=%region_5.6 | all-reduce | flops 1 | bytes 8 | tf_op jit(solution)/shard_map/psum | solution.py:147
  655.7 0.8 fusion.29
  656.5 0.8 fusion.20
  660.3 0.9 subtract_bitcast_fusion
  661.2 0.8 copy.19
  662.0 6.5 all-to-all-start.6
  668.6 12.2 %all-to-all-done.6 = f32[2,1,1,128,128]{4,2,1,0,3:T(1,128)S(1)} async-done(((f32[2,1,1,128,128]{4,2,1,0,3:T(1,128)}), f32[2,1,1,128,128]{4,2,1,0,3:T(1,128)S(1)}, u32[]{:S(2)}, u32[]{:S(2)}) %all-to-all-start.6) | async-done | bytes 131104 | tf_op jit(solution)/shard_map/all_to_all | solution.py:95
  682.8 12.5 %all-gather = f32[512,128]{1,0:T(8,128)S(1)} all-gather(f32[128,128]{1,0:T(8,128)S(1)} %fusion.21), channel_id=2, replica_groups=mesh['probe'=4,'seq'=128] {'probe'}, dimensions={0}, use_global_device_ids=true | all-gather | bytes 327680 | tf_op jit(solution)/shard_map/all_gather | solution.py:12
  (96 shorter events, 38.3 us)
Async XLA Ops:
  36.6 0.8 copy-start.4
  85.7 0.8 copy-start.2
  110.7 0.8 copy-start.3
  362.8 293.7 %copy-start = (f32[128,128]{1,0:T(8,128)}, f32[128,128]{1,0:T(8,128)S(1)}, u32[]{:S(2)}) copy-start(f32[128,128]{1,0:T(8,128)S(1)} %get-tuple-element.9) | copy-start | bytes 196612
  391.1 261.5 %all-to-all-start.5 = ((f32[2,1,128,1,128]{4,3,1,0,2:T(1,128)}), f32[2,1,128,1,128]{4,3,1,0,2:T(1,128)S(1)}, u32[]{:S(2)}, u32[]{:S(2)}) async-start(f32[2,1,128,1,128]{4,3,1,0,2:T(1,128)} %copy.16), calls=%async_computation.5 | async-start | bytes 262144 | tf_op jit(solution)/shard_map/all_to_all | solution.py:117
  662.0 6.5 copy-start.1
  662.0 18.8 %all-to-all-start.6 = ((f32[2,1,1,128,128]{4,2,1,0,3:T(1,128)}), f32[2,1,1,128,128]{4,2,1,0,3:T(1,128)S(1)}, u32[]{:S(2)}, u32[]{:S(2)}) async-start(f32[2,1,1,128,128]{4,2,1,0,3:T(1,128)} %copy.19), calls=%async_computation.6 | async-start | bytes 262144 | tf_op jit(solution)/shard_map/all_to_all | solution.py:95
